TPU v7x, 32 devices: a whole 2x2x4 slice. The times are simulated.
32 devices in a mesh: rep: 8 (over z, core), tp: 4 (over y, x).
Axes of the slice: x: 2, y: 2, z: 4, core: 2. Of those that a mesh axis runs over, the one named last changes fastest.
Arguments:
- hidden: bfloat16 [32, 4608], P('rep'), may hold values from -6 to 6
- positions: int32 [32], P('rep'), may hold values from 1 to 1023
- key_cache: bfloat16 [32, 16, 1024, 128], P('rep', 'tp'), may hold values from -6 to 6
- value_cache: bfloat16 [32, 16, 1024, 128], P('rep', 'tp'), may hold values from -6 to 6
- norm_gain: float32 [4608], replicated, may hold values from 0.1 to 1.9
- q_proj: bfloat16 [4096, 4608], P(('rep', 'tp')), may hold values from -0.09375 to 0.09375
- k_proj: bfloat16 [2048, 4608], P(('rep', 'tp')), may hold values from -0.09375 to 0.09375
- v_proj: bfloat16 [2048, 4608], P(('rep', 'tp')), may hold values from -0.09375 to 0.09375
- o_proj: bfloat16 [4608, 4096], P(('rep', 'tp')), may hold values from -0.09375 to 0.09375
- post_gain: float32 [4608], P('tp'), may hold values from 0.1 to 1.9
Outputs:
- joined_qkv: bfloat16 [4608, 8192], P(None, 'tp')
- wo_heads: bfloat16 [4096, 4608], P('tp')
- attn_out: bfloat16 [32, 4608], P('rep', 'tp')
All inputs are finite; a program needn't handle non-finite values.
Results may differ from a plain program's by a relative error of at most 0.008.
Values may be sent and summed in bfloat16 or wider, within the bound.
A program may use at most 128 MiB of HBM per device.

v0:
```python
import jax
import jax.numpy as jnp
from jax import lax
from jax.sharding import PartitionSpec as P

score_scale = 144.0 ** (-0.5)
soft_cap = 50.0


def rms_scale(values, gain):
    mean_square = jnp.mean(values * values, axis=-1, keepdims=True)
    return values * lax.rsqrt(mean_square + 1e-06) * gain


def rotate(values, positions):
    half = values.shape[-1] // 2
    freq = 10000.0 ** (-2.0 * jnp.arange(half, dtype=jnp.float32) / values.shape[-1])
    angle = positions.astype(jnp.float32)[:, None] * freq[None, :]
    cosine = jnp.cos(angle)[:, None, :]
    sine = jnp.sin(angle)[:, None, :]
    first = values[..., :half]
    second = values[..., half:]
    return jnp.concatenate(
        [first * cosine - second * sine, second * cosine + first * sine], axis=-1
    )


def body(
    hidden, positions, key_cache, value_cache, norm_gain, q_proj, k_proj, v_proj, o_proj, post_gain
):
    tp_count = lax.axis_size("tp")
    replica_count = lax.axis_size("rep")
    per_tp = replica_count // tp_count
    model_width = hidden.shape[1]
    stacked = (
        lax.all_gather(q_proj[None], "rep", axis=0, tiled=True),
        lax.all_gather(k_proj[None], "rep", axis=0, tiled=True),
        lax.all_gather(v_proj[None], "rep", axis=0, tiled=True),
    )
    shaped = [matrix.reshape((tp_count, per_tp, 1) + matrix.shape[1:]) for matrix in stacked]
    arrived = (
        lax.all_to_all(shaped[0], "tp", split_axis=0, concat_axis=2, tiled=True),
        lax.all_to_all(shaped[1], "tp", split_axis=0, concat_axis=2, tiled=True),
        lax.all_to_all(shaped[2], "tp", split_axis=0, concat_axis=2, tiled=True),
    )
    head_block = [matrix.reshape(-1, model_width) for matrix in arrived]
    joined_block = jnp.transpose(jnp.concatenate(head_block, axis=0))
    split_cols = o_proj.reshape(o_proj.shape[0], tp_count, -1)
    rows_of_group = lax.all_to_all(split_cols, "tp", split_axis=1, concat_axis=0, tiled=True)
    complete_rows = lax.all_gather(rows_of_group, "rep", axis=0, tiled=True)
    out_block = jnp.transpose(complete_rows.reshape(model_width, -1))
    batch, kv_local, length, head_dim = key_cache.shape
    q_width = head_block[0].shape[0]
    kv_width = head_block[1].shape[0]
    q_local = q_width // head_dim
    group = q_local // kv_local
    normed = rms_scale(hidden.astype(jnp.float32), norm_gain).astype(jnp.bfloat16)
    query_key_value_projected = jnp.dot(normed, joined_block, preferred_element_type=jnp.float32)
    query = query_key_value_projected[:, :q_width].reshape(batch, q_local, head_dim)
    keys_new = query_key_value_projected[:, q_width : q_width + kv_width].reshape(
        batch, kv_local, head_dim
    )
    values_new = query_key_value_projected[:, q_width + kv_width :].reshape(
        batch, kv_local, head_dim
    )
    query_rot = rotate(query, positions).astype(jnp.bfloat16)
    rotated_keys = rotate(keys_new, positions).astype(jnp.bfloat16)
    values_rot = values_new.astype(jnp.bfloat16)
    grouped_heads = query_rot.reshape(batch, kv_local, group, head_dim)
    scores = (
        jnp.einsum("bkgd,bkld->bkgl", grouped_heads, key_cache, preferred_element_type=jnp.float32)
        * score_scale
    )
    capped = soft_cap * jnp.tanh(scores / soft_cap)
    valid = jnp.arange(length, dtype=jnp.int32)[None, :] < positions[:, None]
    weight_raw = jnp.where(valid[:, None, None, :], jnp.exp(capped), 0.0)
    self_score = (
        jnp.einsum("juzy,juy->juz", grouped_heads, rotated_keys, preferred_element_type=jnp.float32)
        * score_scale
    )
    self_raw = jnp.exp(soft_cap * jnp.tanh(self_score / soft_cap))
    denom = jnp.sum(weight_raw, axis=-1) + self_raw
    weights = (weight_raw / denom[..., None]).astype(jnp.bfloat16)
    self_weight = (self_raw / denom).astype(jnp.bfloat16)
    attention = jnp.einsum(
        "bkgl,bkld->bkgd", weights, value_cache, preferred_element_type=jnp.float32
    )
    attention = (
        attention
        + self_weight.astype(jnp.float32)[..., None] * values_rot.astype(jnp.float32)[:, :, None, :]
    )
    attention = attention.reshape(batch, q_width).astype(jnp.bfloat16)
    partial_out = jnp.dot(attention, out_block, preferred_element_type=jnp.float32)
    width_local = post_gain.shape[0]
    total = lax.psum(partial_out, "tp")
    multiplier = lax.rsqrt(jnp.mean(total * total, axis=1) + 1e-06)
    share = lax.dynamic_slice_in_dim(total, lax.axis_index("tp") * width_local, width_local, 1)
    result = share * multiplier[:, None] * post_gain
    return (joined_block, out_block, result.astype(jnp.bfloat16))


def solution(mesh):
    in_specs = (
        P("rep", None),
        P("rep"),
        P("rep", "tp", None, None),
        P("rep", "tp", None, None),
        P(),
        P(("rep", "tp"), None),
        P(("rep", "tp"), None),
        P(("rep", "tp"), None),
        P(("rep", "tp"), None),
        P("tp"),
    )
    out_specs = (P(None, "tp"), P("tp", None), P("rep", "tp"))
    return jax.shard_map(body, mesh=mesh, in_specs=in_specs, out_specs=out_specs, check_vma=False)
```

profile of v0, /device:TPU:0, one launch (start us, length us, event | category | flops | bytes accessed | tf_op | source)
XLA Modules:
  0.0 437.0 jit_solution(3041150683269415164)
XLA Ops:
  9.4 1.4 copy.53
  10.8 20.6 %all_to_all.63 = bf16[144,4,1024]{2,0,1:T(8,128)(2,1)} all-to-all(bf16[144,4,1024]{2,0,1:T(8,128)(2,1)S(1)} %bitcast.63), channel_id=1, replica_groups=mesh['rep'=8,'tp'=4] {'tp'}, dimensions={1} | all-to-all | bytes 2359296 | tf_op jit(solution)/shard_map/all_to_all | solution.py:49
  31.5 32.1 %all-gather.14.cloned.1.call-done = bf16[512,4608]{1,0:T(8,128)(2,1)} async-done(((bf16[64,4608]{1,0:T(8,128)(2,1)}), bf16[512,4608]{1,0:T(8,128)(2,1)}) %all-gather.14.cloned.1.call-update) | async-done | bytes 4718608 | tf_op jit(solution)/shard_map/all_gather | solution.py:38
  63.6 5.0 %all-to-all-start.2 = ((bf16[4,2,1,64,4608]{4,3,1,2,0:T(8,128)(2,1)}), bf16[4,2,1,64,4608]{4,3,1,2,0:T(8,128)(2,1)}, u32[]{:S(2)}, u32[]{:S(2)}) async-start(bf16[4,2,1,64,4608]{4,3,1,2,0:T(8,128)(2,1)} %bitcast.61), calls=%async_computation.2 | async-start | bytes 9437184 | tf_op jit(solution)/shard_map/all_to_all | solution.py:44
  68.5 46.7 %all-gather.12.cloned.1.call-done = bf16[512,4608]{1,0:T(8,128)(2,1)} async-done(((bf16[64,4608]{1,0:T(8,128)(2,1)}), bf16[512,4608]{1,0:T(8,128)(2,1)}) %all-gather.12.cloned.1.call-update) | async-done | bytes 4718608 | tf_op jit(solution)/shard_map/all_gather | solution.py:37
  115.2 7.0 %all-to-all-done.2 = bf16[4,2,1,64,4608]{4,3,1,2,0:T(8,128)(2,1)} async-done(((bf16[4,2,1,64,4608]{4,3,1,2,0:T(8,128)(2,1)}), bf16[4,2,1,64,4608]{4,3,1,2,0:T(8,128)(2,1)}, u32[]{:S(2)}, u32[]{:S(2)}) %all-to-all-start.2) | async-done | bytes 4718624 | tf_op jit(solution)/shard_map/all_to_all | solution.py:44
  122.2 5.0 %all-to-all-start.1 = ((bf16[4,2,1,64,4608]{4,3,1,2,0:T(8,128)(2,1)}), bf16[4,2,1,64,4608]{4,3,1,2,0:T(8,128)(2,1)}, u32[]{:S(2)}, u32[]{:S(2)}) async-start(bf16[4,2,1,64,4608]{4,3,1,2,0:T(8,128)(2,1)} %bitcast.60), calls=%async_computation.1 | async-start | bytes 9437184 | tf_op jit(solution)/shard_map/all_to_all | solution.py:43
  127.3 79.1 %all-gather.10.cloned.1.call-done = bf16[1024,4608]{1,0:T(8,128)(2,1)} async-done(((bf16[128,4608]{1,0:T(8,128)(2,1)}), bf16[1024,4608]{1,0:T(8,128)(2,1)}) %all-gather.10.cloned.1.call-update) | async-done | bytes 9437200 | tf_op jit(solution)/shard_map/all_gather | solution.py:36
  206.4 23.7 %copy.36 = bf16[4,2,1,128,4608]{3,1,4,2,0:T(2,128)(2,1)} copy(bf16[4,2,1,128,4608]{4,3,1,0,2:T(8,128)(2,1)} %bitcast.59) | data formatting | bytes 18874368 | tf_op jit(solution)/shard_map/reshape | solution.py:40
  230.1 6.0 %all-to-all-start = ((bf16[4,2,1,128,4608]{3,1,4,2,0:T(2,128)(2,1)}), bf16[4,2,1,128,4608]{3,1,4,2,0:T(2,128)(2,1)}, u32[]{:S(2)}, u32[]{:S(2)}) async-start(bf16[4,2,1,128,4608]{3,1,4,2,0:T(2,128)(2,1)} %copy.36), calls=%async_computation | async-start | bytes 18874368 | tf_op jit(solution)/shard_map/all_to_all | solution.py:42
  236.6 4.9 %copy.41 = bf16[4,2,1,64,4608]{4,3,0,1,2:T(8,128)(2,1)} copy(bf16[4,2,1,64,4608]{4,3,1,2,0:T(8,128)(2,1)} %all-to-all-done.2) | data formatting | bytes 9437184 | tf_op jit(solution)/shard_map/all_to_all | solution.py:44
  241.4 4.9 %copy.39 = bf16[4,2,1,64,4608]{4,3,0,1,2:T(8,128)(2,1)} copy(bf16[4,2,1,64,4608]{4,3,1,2,0:T(8,128)(2,1)} %all-to-all-done.1) | data formatting | bytes 9437184 | tf_op jit(solution)/shard_map/all_to_all | solution.py:43
  246.3 50.7 %all-gather.8.cloned.1.call-done = bf16[4608,1,1024]{2,0,1:T(8,128)(2,1)} async-done(((bf16[576,1,1024]{2,0,1:T(8,128)(2,1)}), bf16[4608,1,1024]{2,0,1:T(8,128)(2,1)}) %all-gather.8.cloned.1.call-update) | async-done | bytes 9437200 | tf_op jit(solution)/shard_map/all_gather | solution.py:50
  297.0 12.6 %copy.44 = bf16[1024,4608]{1,0:T(8,128)(2,1)} copy(bf16[1024,4608]{0,1:T(8,128)(2,1)} %bitcast.52) | data formatting | bytes 18874368
  309.6 30.8 %all-to-all-done = bf16[4,2,1,128,4608]{3,1,4,2,0:T(2,128)(2,1)} async-done(((bf16[4,2,1,128,4608]{3,1,4,2,0:T(2,128)(2,1)}), bf16[4,2,1,128,4608]{3,1,4,2,0:T(2,128)(2,1)}, u32[]{:S(2)}, u32[]{:S(2)}) %all-to-all-start) | async-done | bytes 9437216 | tf_op jit(solution)/shard_map/all_to_all | solution.py:42
  340.5 23.5 %copy.37 = bf16[4,2,1,128,4608]{4,3,0,1,2:T(8,128)(2,1)} copy(bf16[4,2,1,128,4608]{3,1,4,2,0:T(2,128)(2,1)} %all-to-all-done) | data formatting | bytes 18874368 | tf_op jit(solution)/shard_map/all_to_all | solution.py:42
  363.9 9.2 %fusion.2 = f32[4,2048]{1,0:T(4,128)S(1)} fusion(bf16[512,4608]{1,0:T(8,128)(2,1)} %bitcast.55, bf16[512,4608]{1,0:T(8,128)(2,1)} %bitcast.57, bf16[1024,4608]{1,0:T(8,128)(2,1)} %bitcast.53, bf16[4,4608]{1,0:T(4,128)(2,1)S(1)} %copy-done, f32[4608]{0:T(1024)S(1)} %copy-done.3, f32[4]{0:T(128)S(1)} %add_rsqrt_fusion.1), kind=kOutput, calls=%fused_computation.3 | convolution fusion | flops 132194304 | bytes 18962448 | tf_op jit(solution)/shard_map/dot_general | solution.py:58
  373.6 3.5 fusion.22
  377.2 2.9 fusion.8
  380.1 6.9 %fusion = f32[4,4608]{1,0:T(4,128)} fusion(bf16[4,1024]{1,0:T(4,128)(2,1)S(1)} %convert_element_type.56, bf16[4608,1,1024]{2,0,1:T(8,128)(2,1)} %all-gather.8.cloned.1.call-done), kind=kOutput, calls=%fused_computation.1 | convolution fusion | flops 37748736 | bytes 9519104 | tf_op jit(solution)/shard_map/dot_general | solution.py:93
  387.0 16.4 %fusion.3 = bf16[4608,2048]{0,1:T(8,128)(2,1)} fusion(bf16[512,4608]{1,0:T(8,128)(2,1)} %bitcast.56, bf16[512,4608]{1,0:T(8,128)(2,1)} %bitcast.58, bf16[1024,4608]{1,0:T(8,128)(2,1)} %bitcast.54), kind=kLoop, calls=%fused_computation.4 | loop fusion | flops 56623104 | bytes 37748736 | tf_op jit(solution)/shard_map/transpose | solution.py:47
  403.4 24.6 %copy.43 = bf16[4608,2048]{1,0:T(8,128)(2,1)} copy(bf16[4608,2048]{0,1:T(8,128)(2,1)} %fusion.3) | data formatting | bytes 37748736
  428.0 1.0 multiply_reduce_fusion
  429.1 1.4 multiply_convert_fusion
  (39 shorter events, 3.2 us)
Async XLA Ops:
  7.2 56.4 %all-gather.14.cloned.1.call-start = ((), (), s32[]{:S(2)}) async-start(), calls=%async_computation.8 | async-start | bytes 5308416 | tf_op jit(solution)/shard_map/all_gather | solution.py:38
  7.9 107.3 %all-gather.12.cloned.1.call-start = ((), (), s32[]{:S(2)}) async-start(), calls=%async_computation.7 | async-start | bytes 5308416 | tf_op jit(solution)/shard_map/all_gather | solution.py:37
  8.6 197.7 %all-gather.10.cloned.1.call-start = ((), (), s32[]{:S(2)}) async-start(), calls=%async_computation.6 | async-start | bytes 10616832 | tf_op jit(solution)/shard_map/all_gather | solution.py:36
  9.4 287.6 %all-gather.8.cloned.1.call-start = ((), (), s32[]{:S(2)}) async-start(), calls=%async_computation.4 | async-start | bytes 10616832 | tf_op jit(solution)/shard_map/all_gather | solution.py:50
  63.6 58.7 %all-to-all-start.2 = ((bf16[4,2,1,64,4608]{4,3,1,2,0:T(8,128)(2,1)}), bf16[4,2,1,64,4608]{4,3,1,2,0:T(8,128)(2,1)}, u32[]{:S(2)}, u32[]{:S(2)}) async-start(bf16[4,2,1,64,4608]{4,3,1,2,0:T(8,128)(2,1)} %bitcast.61), calls=%async_computation.2 | async-start | bytes 9437184 | tf_op jit(solution)/shard_map/all_to_all | solution.py:44
  122.2 107.9 %all-to-all-start.1 = ((bf16[4,2,1,64,4608]{4,3,1,2,0:T(8,128)(2,1)}), bf16[4,2,1,64,4608]{4,3,1,2,0:T(8,128)(2,1)}, u32[]{:S(2)}, u32[]{:S(2)}) async-start(bf16[4,2,1,64,4608]{4,3,1,2,0:T(8,128)(2,1)} %bitcast.60), calls=%async_computation.1 | async-start | bytes 9437184 | tf_op jit(solution)/shard_map/all_to_all | solution.py:43
  230.1 6.0 %copy-start.2 = (s32[4]{0:T(128)S(1)}, s32[4]{0:T(128)}, u32[]{:S(2)}) copy-start(s32[4]{0:T(128)} %param.11) | copy-start | bytes 52
  230.1 6.1 %copy-start = (bf16[4,4608]{1,0:T(4,128)(2,1)S(1)}, bf16[4,4608]{1,0:T(4,128)(2,1)}, u32[]{:S(2)}) copy-start(bf16[4,4608]{1,0:T(4,128)(2,1)} %param.10) | copy-start | bytes 110596
  230.1 110.3 %all-to-all-start = ((bf16[4,2,1,128,4608]{3,1,4,2,0:T(2,128)(2,1)}), bf16[4,2,1,128,4608]{3,1,4,2,0:T(2,128)(2,1)}, u32[]{:S(2)}, u32[]{:S(2)}) async-start(bf16[4,2,1,128,4608]{3,1,4,2,0:T(2,128)(2,1)} %copy.36), calls=%async_computation | async-start | bytes 18874368 | tf_op jit(solution)/shard_map/all_to_all | solution.py:42
  236.1 191.9 %all-reduce.2.cloned.1.call-start = ((), (), s32[]{:S(2)}) async-start(), calls=%async_computation.5 | async-start | bytes 147456 | tf_op jit(solution)/shard_map/psum | solution.py:95
  309.6 54.3 %copy-start.3 = (f32[4608]{0:T(1024)S(1)}, f32[4608]{0:T(1024)}, u32[]{:S(2)}) copy-start(f32[4608]{0:T(1024)} %param.14) | copy-start | bytes 55300
  403.4 25.7 %copy-start.1 = (f32[1152]{0:T(1024)S(1)}, f32[1152]{0:T(1024)}, u32[]{:S(2)}) copy-start(f32[1152]{0:T(1024)} %param.19) | copy-start | bytes 13828
Sparse Core Ops, SparseCore 0:
  9.6 53.9 all-gather.13
  65.2 49.9 all-gather.11
  116.9 89.4 all-gather.9
  207.9 89.1 all-gather.7
  387.1 38.0 all-reduce.1
where the time goes:
time: 440 us; the launch traced here: 437 us
  waiting for transfers between devices  249 us (57%)
  local copies, waits for them, and re-layouts  95.6 us (22%)
  matrix products  22.7 us (5%)
  blocking collectives  20.6 us (5%)
  other arithmetic  19.4 us (4%)
  starting transfers between devices  16.1 us (4%)
  between operations  13.9 us (3%)
    all_gather x1, waiting for transfers between devices, body(): lax.all_gather(q_proj[None], 'rep', axis=0, tiled=True)  79.1 us
    all_gather x1, waiting for transfers between devices, body(): complete_rows = lax.all_gather(rows_of_group, 'rep', axis=0, tiled=True)  50.7 us
    all_gather x1, waiting for transfers between devices, body(): lax.all_gather(k_proj[None], 'rep', axis=0, tiled=True)  46.7 us
    unnamed x12, local copies, waits for them, and re-layouts  37.2 us
    all_gather x1, waiting for transfers between devices, body(): lax.all_gather(v_proj[None], 'rep', axis=0, tiled=True)  32.1 us
    all_to_all x1, waiting for transfers between devices, body(): lax.all_to_all(shaped[0], 'tp', split_axis=0, concat_axis=2, tiled=True)  30.8 us
    reshape x1, local copies, waits for them, and re-layouts, body(): matrix.reshape((tp_count, per_tp, 1) + matrix.shape[1:])  23.7 us
    all_to_all x1, local copies, waits for them, and re-layouts, body(): lax.all_to_all(shaped[0], 'tp', split_axis=0, concat_axis=2, tiled=True)  23.5 us
  transfers between devices with their start and end apart: 8, of which 6 were waited for; matrix products, arithmetic and copies ran while one was open for 20% of the time, Pallas kernels for 0%

commit v1 on v0

v1 whole, which is shorter than its diff:
```python
import functools

import jax
import jax.numpy as jnp
from jax import lax
from jax.experimental import pallas as pl
from jax.experimental.pallas import tpu as pltpu
from jax.sharding import PartitionSpec as P

score_scale = 144.0 ** (-0.5)
soft_cap = 50.0


def rms_scale(values, gain):
    mean_square = jnp.mean(values * values, axis=-1, keepdims=True)
    return values * lax.rsqrt(mean_square + 1e-06) * gain


def rotate(values, positions):
    half = values.shape[-1] // 2
    freq = 10000.0 ** (-2.0 * jnp.arange(half, dtype=jnp.float32) / values.shape[-1])
    angle = positions.astype(jnp.float32)[:, None] * freq[None, :]
    cosine = jnp.cos(angle)[:, None, :]
    sine = jnp.sin(angle)[:, None, :]
    first = values[..., :half]
    second = values[..., half:]
    return jnp.concatenate(
        [first * cosine - second * sine, second * cosine + first * sine], axis=-1
    )


def join_kernel(per_tp, q_rows, k_rows, *refs):
    slot = lax.rem(lax.axis_index("rep"), per_tp)
    parts, out_ref = refs[:-1], refs[-1]
    tp_count = parts[0].shape[0]
    q_all = tp_count * per_tp * q_rows
    k_all = tp_count * per_tp * k_rows
    for step in range(per_tp):
        who = lax.rem(slot + step, per_tp)
        q_ref, kv_ref = parts[2 * step], parts[2 * step + 1]
        for start, ref, low, rows in (
            (0, q_ref, 0, q_rows),
            (q_all, kv_ref, 0, k_rows),
            (q_all + k_all, kv_ref, k_rows, k_rows),
        ):
            block = ref[:, low : low + rows, :].reshape(tp_count * rows, -1)
            at = pl.multiple_of(start + who * (tp_count * rows), 128)
            out_ref[:, pl.ds(at, tp_count * rows)] = jnp.transpose(block)


def join(per_tp, pairs):
    tp_count, q_rows, width = pairs[0][0].shape
    k_rows = pairs[0][1].shape[1] // 2
    columns = tp_count * per_tp * (q_rows + 2 * k_rows)
    stripe = 256
    operands, specs = [], []
    for pair in pairs:
        for matrix in pair:
            operands.append(matrix)
            specs.append(
                pl.BlockSpec((tp_count, matrix.shape[1], stripe), lambda j: (0, 0, j))
            )
    size = width * columns * 2
    return pl.pallas_call(
        functools.partial(join_kernel, per_tp, q_rows, k_rows),
        grid=(width // stripe,),
        in_specs=specs,
        out_specs=pl.BlockSpec((stripe, columns), lambda j: (j, 0)),
        out_shape=jax.ShapeDtypeStruct((width, columns), jnp.bfloat16),
        cost_estimate=pl.CostEstimate(flops=0, bytes_accessed=2 * size, transcendentals=0),
        name="join",
    )(*operands)


def body(
    hidden, positions, key_cache, value_cache, norm_gain, q_proj, k_proj, v_proj, o_proj, post_gain
):
    tp_count = lax.axis_size("tp")
    replica_count = lax.axis_size("rep")
    per_tp = replica_count // tp_count
    model_width = hidden.shape[1]
    q_rows, k_rows = q_proj.shape[0], k_proj.shape[0]

    groups = [[i + per_tp * p for p in range(tp_count)] for i in range(per_tp)]
    shifts = [
        [
            (per_tp * p + (i + d) % per_tp, per_tp * p + i)
            for p in range(tp_count)
            for i in range(per_tp)
        ]
        for d in range(1, per_tp)
    ]

    def collect(rows):
        planes = lax.all_gather(rows[None], "rep", axis=0, tiled=True, axis_index_groups=groups)
        return lax.all_to_all(planes, "tp", split_axis=0, concat_axis=0, tiled=True)

    kv_rows = collect(jnp.concatenate([k_proj, v_proj], axis=0))
    split_cols = o_proj.reshape(o_proj.shape[0], tp_count, -1)
    rows_of_group = lax.all_to_all(split_cols, "tp", split_axis=1, concat_axis=0, tiled=True)

    batch, kv_local, length, head_dim = key_cache.shape

    def scatter_rows(values):
        wide = values.reshape(replica_count, batch, -1)
        by_rep = lax.all_to_all(wide, "rep", split_axis=0, concat_axis=0, tiled=True)
        return by_rep

    def to_block(by_rep):
        arrived = lax.all_to_all(by_rep, "tp", split_axis=0, concat_axis=0, tiled=True)
        arrived = arrived.reshape(tp_count, per_tp, batch, -1)
        return jnp.transpose(arrived, (2, 1, 0, 3))

    normed = rms_scale(hidden.astype(jnp.float32), norm_gain).astype(jnp.bfloat16)
    normed_all = lax.all_gather(normed, "rep", axis=0, tiled=True)
    contract = (((1,), (1,)), ((), ()))
    local = jnp.concatenate(
        [
            lax.dot_general(normed_all, matrix, contract, preferred_element_type=jnp.float32)
            for matrix in (q_proj, k_proj, v_proj)
        ],
        axis=1,
    )
    block = to_block(scatter_rows(local))
    q_local = tp_count * per_tp * q_rows // head_dim
    group = q_local // kv_local
    query = block[..., :q_rows].reshape(batch, q_local, head_dim)
    keys_new = block[..., q_rows : q_rows + k_rows].reshape(batch, kv_local, head_dim)
    values_new = block[..., q_rows + k_rows :].reshape(batch, kv_local, head_dim)
    query_rot = rotate(query, positions).astype(jnp.bfloat16)
    rotated_keys = rotate(keys_new, positions).astype(jnp.bfloat16)
    values_rot = values_new.astype(jnp.bfloat16)
    grouped_heads = query_rot.reshape(batch, kv_local, group, head_dim)
    scores = (
        jnp.einsum("bkgd,bkld->bkgl", grouped_heads, key_cache, preferred_element_type=jnp.float32)
        * score_scale
    )
    capped = soft_cap * jnp.tanh(scores / soft_cap)
    valid = jnp.arange(length, dtype=jnp.int32)[None, :] < positions[:, None]
    weight_raw = jnp.where(valid[:, None, None, :], jnp.exp(capped), 0.0)
    self_score = (
        jnp.einsum("juzy,juy->juz", grouped_heads, rotated_keys, preferred_element_type=jnp.float32)
        * score_scale
    )
    self_raw = jnp.exp(soft_cap * jnp.tanh(self_score / soft_cap))
    denom = jnp.sum(weight_raw, axis=-1) + self_raw
    weights = (weight_raw / denom[..., None]).astype(jnp.bfloat16)
    self_weight = (self_raw / denom).astype(jnp.bfloat16)
    attention = jnp.einsum(
        "bkgl,bkld->bkgd", weights, value_cache, preferred_element_type=jnp.float32
    )
    attention = (
        attention
        + self_weight.astype(jnp.float32)[..., None] * values_rot.astype(jnp.float32)[:, :, None, :]
    )
    attention = attention.reshape(batch, q_local * head_dim).astype(jnp.bfloat16)
    q_later, attention = lax.optimization_barrier((q_proj, attention))
    q_own = collect(q_later)
    pairs = [(q_own, kv_rows)]
    for shift in shifts:
        pairs.append((lax.ppermute(q_own, "rep", shift), lax.ppermute(kv_rows, "rep", shift)))
    joined_block = join(per_tp, pairs)
    own_all = lax.all_gather(attention, "tp", axis=1, tiled=True)
    attention_all = lax.all_gather(own_all, "rep", axis=0, tiled=True)
    projected = lax.dot_general(
        attention_all, o_proj, contract, preferred_element_type=jnp.float32
    )
    by_rep = scatter_rows(projected)
    share = to_block(by_rep).reshape(batch, -1)
    square = jnp.sum(share * share, axis=1)
    square_all = lax.all_gather(square[None], "tp", axis=0, tiled=True)
    multiplier = lax.rsqrt(jnp.sum(square_all, axis=0) / model_width + 1e-06)
    result = share * multiplier[:, None] * post_gain
    rows_of_group, result = lax.optimization_barrier((rows_of_group, result))
    complete_rows = lax.all_gather(rows_of_group, "rep", axis=0, tiled=True)
    out_block = jnp.transpose(complete_rows.reshape(model_width, -1))
    return (joined_block, out_block, result.astype(jnp.bfloat16))


def solution(mesh):
    in_specs = (
        P("rep", None),
        P("rep"),
        P("rep", "tp", None, None),
        P("rep", "tp", None, None),
        P(),
        P(("rep", "tp"), None),
        P(("rep", "tp"), None),
        P(("rep", "tp"), None),
        P(("rep", "tp"), None),
        P("tp"),
    )
    out_specs = (P(None, "tp"), P("tp", None), P("rep", "tp"))
    return jax.shard_map(body, mesh=mesh, in_specs=in_specs, out_specs=out_specs, check_vma=False)
```

time: 440 us -> 307 us (0.70)
  waiting for transfers between devices: 249 us -> 148 us
  local copies, waits for them, and re-layouts: 95.6 us -> 16.9 us
  blocking collectives: 20.6 us -> 66.7 us
  Pallas kernels: 0 us -> 21.4 us
  matrix products: 22.7 us -> 6.16 us
  other arithmetic: 19.4 us -> 5.75 us
  starting transfers between devices: 16.1 us -> 25.7 us
    all_gather x3 -> x2, waiting for transfers between devices: 158 us -> 67.4 us  [collect(): lax.all_gather(rows[None], 'rep', axis=0, tiled=True, axis_index_groups=g...]
    all_gather x1, waiting for transfers between devices: 50.7 us -> 2.27 us  [body(): complete_rows = lax.all_gather(rows_of_group, 'rep', axis=0, tiled=True)]
    all_gather x0 -> x3, blocking collectives: none -> 40.5 us  [the longest x1 16.7 us: body(): attention_all = lax.all_gather(own_all, 'rep', axis=0, tiled=True)]
    all_to_all x3 -> x0, local copies, waits for them, and re-layouts: 33.2 us -> none  [the longest x1 23.5 us: body(): lax.all_to_all(shaped[0], 'tp', split_axis=0, concat_axis=2, tiled=True)]
    all_to_all x3 -> x6, waiting for transfers between devices: 37.9 us -> 69.6 us  [the longest x2 53.2 us: collect(): return lax.all_to_all(planes, 'tp', split_axis=0, concat_axis=0, tiled=True)]
    reshape x2 -> x5, local copies, waits for them, and re-layouts: 23.8 us -> 0.87 us  [the longest x2 0.67 us: scatter_rows(): wide = values.reshape(replica_count, batch, -1)]
    unnamed x12 -> x24, local copies, waits for them, and re-layouts: 37.2 us -> 14.7 us
    pallas_call x0 -> x1, Pallas kernels: none -> 21.4 us  [join(): pl.pallas_call(functools.partial(join_kernel, per_tp, q_rows, k_rows), gr...]
  transfers between devices with their start and end apart: 8 -> 11, of which waited for: 6 -> 7; matrix products, arithmetic and copies ran while one was open for 20% -> 4% of each run, Pallas kernels for 0% -> 7%
where the time goes in v1:
time: 307 us; the launch traced here: 305 us
  waiting for transfers between devices  148 us (48%)
  blocking collectives  66.7 us (22%)
  starting transfers between devices  25.7 us (8%)
  Pallas kernels  21.4 us (7%)
  local copies, waits for them, and re-layouts  16.9 us (6%)
  between operations  14.6 us (5%)
  matrix products  6.16 us (2%)
  other arithmetic  5.75 us (2%)
    all_gather x2, waiting for transfers between devices, collect(): lax.all_gather(rows[None], 'rep', axis=0, tiled=True, axis_index_groups=g...  67.4 us
    all_to_all x2, waiting for transfers between devices, collect(): return lax.all_to_all(planes, 'tp', split_axis=0, concat_axis=0, tiled=True)  53.2 us
    pallas_call x1, Pallas kernels, join(): pl.pallas_call(functools.partial(join_kernel, per_tp, q_rows, k_rows), gr...  21.4 us
    all_gather x1, blocking collectives, body(): attention_all = lax.all_gather(own_all, 'rep', axis=0, tiled=True)  16.7 us
    all_gather x1, blocking collectives, body(): normed_all = lax.all_gather(normed, 'rep', axis=0, tiled=True)  16.5 us
    unnamed x1, blocking collectives  16 us
    unnamed x24, local copies, waits for them, and re-layouts  14.7 us
    all_to_all x1, blocking collectives, scatter_rows(): lax.all_to_all(wide, 'rep', split_axis=0, concat_axis=0, tiled=True)  10.2 us
  transfers between devices with their start and end apart: 11, of which 7 were waited for; matrix products, arithmetic and copies ran while one was open for 4% of the time, Pallas kernels for 7%

profile of v1, /device:TPU:0, one launch (start us, length us, event | category | flops | bytes accessed | tf_op | source)
XLA Modules:
  0.0 305.4 jit_solution(9626119585714235028)
XLA Ops:
  7.3 2.5 pad_maximum_fusion
  11.6 16.5 %all-gather.3 = bf16[8,4,4608]{2,1,0:T(4,128)(2,1)S(1)} all-gather(bf16[1,4,4608]{2,1,0:T(4,128)(2,1)S(1)} %fusion.9), channel_id=1, replica_groups=mesh['rep'=8,'tp'=4] {'rep'}, dimensions={0}, use_global_device_ids=true | all-gather | bytes 331776 | tf_op jit(solution)/shard_map/all_gather | solution.py:115
  29.9 5.2 %all-to-all-start = ((f32[8,4,256]{2,1,0:T(4,128)}), f32[8,4,256]{2,1,0:T(4,128)}, u32[]{:S(2)}, u32[]{:S(2)}) async-start(f32[8,4,256]{2,1,0:T(4,128)} %reshape.134), calls=%async_computation | async-start | bytes 65536 | tf_op jit(solution)/shard_map/all_to_all | solution.py:106
  35.3 8.2 %all-to-all-done = f32[8,4,256]{2,1,0:T(4,128)} async-done(((f32[8,4,256]{2,1,0:T(4,128)}), f32[8,4,256]{2,1,0:T(4,128)}, u32[]{:S(2)}, u32[]{:S(2)}) %all-to-all-start) | async-done | bytes 32800 | tf_op jit(solution)/shard_map/all_to_all | solution.py:106
  43.4 3.6 %all-to-all-start.1 = ((f32[8,4,256]{2,1,0:T(4,128)}), f32[8,4,256]{2,1,0:T(4,128)S(1)}, u32[]{:S(2)}, u32[]{:S(2)}) async-start(f32[8,4,256]{2,1,0:T(4,128)} %all-to-all-done), calls=%async_computation.1 | async-start | bytes 65536 | tf_op jit(solution)/shard_map/all_to_all | solution.py:110
  47.2 4.7 %all-to-all-done.1 = f32[8,4,256]{2,1,0:T(4,128)S(1)} async-done(((f32[8,4,256]{2,1,0:T(4,128)}), f32[8,4,256]{2,1,0:T(4,128)S(1)}, u32[]{:S(2)}, u32[]{:S(2)}) %all-to-all-start.1) | async-done | bytes 32800 | tf_op jit(solution)/shard_map/all_to_all | solution.py:110
  52.6 3.8 %fusion.15 = (f32[4,4,2]{2,1,0:T(4,128)S(1)}, f32[4,4,2,1024]{3,2,1,0:T(2,128)S(1)}) fusion(bf16[4,4,1024,128]{3,2,1,0:T(8,128)(2,1)} %param.12, bf16[4,4,2,64]{3,2,1,0:T(2,128)(2,1)S(1)} %bitcast.60, bf16[4,4,2,64]{3,2,1,0:T(2,128)(2,1)S(1)} %bitcast.58, pred[4,1024]{1,0:T(4,128)(4,1)S(1)} %iota_compare_fusion), kind=kOutput, calls=%fused_computation.41 | convolution fusion | flops 8536032 | bytes 4337792 | tf_op jit(solution)/shard_map/bkgd,bkld->bkgl/dot_general | solution.py:135
  57.2 7.3 %all_gather.24 = bf16[4,4096]{1,0:T(4,128)(2,1)S(1)} all-gather(bf16[4,1024]{1,0:T(4,128)(2,1)S(1)} %convert_element_type.56), channel_id=1, replica_groups=mesh['rep'=8,'tp'=4] {'tp'}, dimensions={1}, use_global_device_ids=true | all-gather | bytes 40960 | tf_op jit(solution)/shard_map/all_gather | solution.py:163
  64.5 16.7 %all-gather.4 = bf16[8,4,4096]{2,1,0:T(4,128)(2,1)S(1)} all-gather(bf16[1,4,4096]{2,1,0:T(4,128)(2,1)S(1)} %bitcast.55), channel_id=1, replica_groups=mesh['rep'=8,'tp'=4] {'rep'}, dimensions={0}, use_global_device_ids=true | all-gather | bytes 294912 | tf_op jit(solution)/shard_map/all_gather | solution.py:164
  81.7 10.2 %all_to_all.48 = f32[8,4,144]{2,1,0:T(4,128)} all-to-all(f32[8,4,144]{2,1,0:T(4,128)S(1)} %reshape.139), channel_id=1, replica_groups=mesh['rep'=8,'tp'=4] {'rep'}, dimensions={0} | all-to-all | bytes 36864 | tf_op jit(solution)/shard_map/all_to_all | solution.py:106
  92.0 3.3 %all-to-all-start.6 = ((f32[8,4,144]{2,1,0:T(4,128)}), f32[8,4,144]{2,1,0:T(4,128)S(1)}, u32[]{:S(2)}, u32[]{:S(2)}) async-start(f32[8,4,144]{2,1,0:T(4,128)} %all_to_all.48), calls=%async_computation.6 | async-start | bytes 65536 | tf_op jit(solution)/shard_map/all_to_all | solution.py:110
  95.3 1.1 copy.44
  96.4 3.6 %all-to-all-done.6 = f32[8,4,144]{2,1,0:T(4,128)S(1)} async-done(((f32[8,4,144]{2,1,0:T(4,128)}), f32[8,4,144]{2,1,0:T(4,128)S(1)}, u32[]{:S(2)}, u32[]{:S(2)}) %all-to-all-start.6) | async-done | bytes 18464 | tf_op jit(solution)/shard_map/all_to_all | solution.py:110
  100.0 3.5 %all-to-all-start.4 = ((bf16[144,4,1024]{2,0,1:T(8,128)(2,1)}), bf16[144,4,1024]{2,0,1:T(8,128)(2,1)S(1)}, u32[]{:S(2)}, u32[]{:S(2)}) async-start(bf16[144,4,1024]{2,0,1:T(8,128)(2,1)} %bitcast.42), calls=%async_computation.4 | async-start | bytes 2359296 | tf_op jit(solution)/shard_map/all_to_all | solution.py:100
  105.2 16.0 %all-reduce = f32[16]{0:T(128)S(1)} all-reduce(f32[16]{0:T(128)S(1)} %dynamic-update-slice), channel_id=4, replica_groups=mesh['rep'=8,'tp'=4] {'tp'}, use_global_device_ids=true, to_apply=%add | all-reduce | flops 16 | bytes 128
  122.0 1.1 copy-done.2
  123.2 5.0 %all-to-all-start.3 = ((bf16[4,128,4608]{2,1,0:T(8,128)(2,1)}), bf16[4,128,4608]{2,1,0:T(8,128)(2,1)}, u32[]{:S(2)}, u32[]{:S(2)}) async-start(bf16[4,128,4608]{2,1,0:T(8,128)(2,1)} %bitcast.45), calls=%async_computation.3 | async-start | bytes 9437184 | tf_op jit(solution)/shard_map/all_to_all | solution.py:96
  128.1 67.3 %all-gather.11.cloned.1.call-done = bf16[512,4608]{1,0:T(8,128)(2,1)} async-done(((bf16[128,4608]{1,0:T(8,128)(2,1)}), bf16[512,4608]{1,0:T(8,128)(2,1)}) %all-gather.11.cloned.1.call-update) | async-done | bytes 4718608 | tf_op jit(solution)/shard_map/all_gather | solution.py:95
  195.5 4.9 %all-to-all-start.2 = ((bf16[4,128,4608]{2,1,0:T(8,128)(2,1)}), bf16[4,128,4608]{2,1,0:T(8,128)(2,1)}, u32[]{:S(2)}, u32[]{:S(2)}) async-start(bf16[4,128,4608]{2,1,0:T(8,128)(2,1)} %bitcast.46), calls=%async_computation.2 | async-start | bytes 9437184 | tf_op jit(solution)/shard_map/all_to_all | solution.py:96
  200.5 53.2 %all-to-all-done.2.refs_0_ = bf16[4,128,4608]{2,1,0:T(8,128)(2,1)} async-done(((bf16[4,128,4608]{2,1,0:T(8,128)(2,1)}), bf16[4,128,4608]{2,1,0:T(8,128)(2,1)}, u32[]{:S(2)}, u32[]{:S(2)}) %all-to-all-start.2) | async-done | bytes 4718624 | tf_op jit(solution)/shard_map/all_to_all | solution.py:96
  253.7 8.9 %collective-permute-done.refs_2_ = bf16[4,128,4608]{2,1,0:T(8,128)(2,1)} collective-permute-done((bf16[4,128,4608]{2,1,0:T(8,128)(2,1)}, bf16[4,128,4608]{2,1,0:T(8,128)(2,1)}, u32[]{:S(2)}, u32[]{:S(2)}) %collective-permute-start) | collective-permute-done | bytes 4718624 | tf_op jit(solution)/shard_map/ppermute | solution.py:161
  262.5 21.4 %join.1 = bf16[4608,2048]{1,0:T(8,128)(2,1)} custom-call(bf16[4,128,4608]{2,1,0:T(8,128)(2,1)} %all-to-all-done.2.refs_0_, bf16[4,128,4608]{2,1,0:T(8,128)(2,1)} %all-to-all-done.3.refs_1_, bf16[4,128,4608]{2,1,0:T(8,128)(2,1)} %collective-permute-done.refs_2_, bf16[4,128,4608]{2,1,0:T(8,128)(2,1)} %collective-permute-done.1.refs_3_), custom_call_target="tpu_custom_call" | custom-call | bytes 37748736 | tf_op jit(solution)/shard_map/join/pallas_call | solution.py:64
  284.0 2.3 all-gather.9.cloned.1.call-done
  286.3 12.6 %copy.34 = bf16[1024,4608]{1,0:T(8,128)(2,1)} copy(bf16[1024,4608]{0,1:T(8,128)(2,1)} %bitcast.44) | data formatting | bytes 18874368
  (70 shorter events, 8.0 us)
Async XLA Ops:
  7.2 21.0 %copy-start.3 = (bf16[64,4608]{1,0:T(8,128)(2,1)S(1)}, bf16[64,4608]{1,0:T(8,128)(2,1)}, u32[]{:S(2)}) copy-start(bf16[64,4608]{1,0:T(8,128)(2,1)} %param.16) | copy-start | bytes 1769476
  7.2 21.2 %copy-start.4 = (bf16[64,4608]{1,0:T(8,128)(2,1)S(1)}, bf16[64,4608]{1,0:T(8,128)(2,1)}, u32[]{:S(2)}) copy-start(bf16[64,4608]{1,0:T(8,128)(2,1)} %param.17) | copy-start | bytes 1769476
  7.2 21.5 %copy-start.1 = (bf16[128,4608]{1,0:T(8,128)(2,1)S(1)}, bf16[128,4608]{1,0:T(8,128)(2,1)}, u32[]{:S(2)}) copy-start(bf16[128,4608]{1,0:T(8,128)(2,1)} %param.15) | copy-start | bytes 3538948
  7.2 27.9 %copy-start.6 = (s32[4]{0:T(128)S(1)}, s32[4]{0:T(128)}, u32[]{:S(2)}) copy-start(s32[4]{0:T(128)} %param.11) | copy-start | bytes 52
  7.2 116.0 %all-gather.13.cloned.1.call-start = ((), (), s32[]{:S(2)}) async-start(), calls=%async_computation.9 | async-start | bytes 5898240 | tf_op jit(solution)/shard_map/all_gather | solution.py:95
  29.9 13.5 %all-to-all-start = ((f32[8,4,256]{2,1,0:T(4,128)}), f32[8,4,256]{2,1,0:T(4,128)}, u32[]{:S(2)}, u32[]{:S(2)}) async-start(f32[8,4,256]{2,1,0:T(4,128)} %reshape.134), calls=%async_computation | async-start | bytes 65536 | tf_op jit(solution)/shard_map/all_to_all | solution.py:106
  43.4 8.4 %all-to-all-start.1 = ((f32[8,4,256]{2,1,0:T(4,128)}), f32[8,4,256]{2,1,0:T(4,128)S(1)}, u32[]{:S(2)}, u32[]{:S(2)}) async-start(f32[8,4,256]{2,1,0:T(4,128)} %all-to-all-done), calls=%async_computation.1 | async-start | bytes 65536 | tf_op jit(solution)/shard_map/all_to_all | solution.py:110
  47.1 148.4 %all-gather.11.cloned.1.call-start = ((), (), s32[]{:S(2)}) async-start(), calls=%async_computation.8 | async-start | bytes 5898240 | tf_op jit(solution)/shard_map/all_gather | solution.py:95
  52.1 4.2 %copy-start.7 = (bf16[4,4,1024,128]{3,2,1,0:T(8,128)(2,1)S(1)}, bf16[4,4,1024,128]{3,2,1,0:T(8,128)(2,1)}, u32[]{:S(2)}) copy-start(bf16[4,4,1024,128]{3,2,1,0:T(8,128)(2,1)} %param.13) | copy-start | bytes 12582916
  56.3 24.9 %copy-start = (bf16[144,4096]{1,0:T(8,128)(2,1)S(1)}, bf16[144,4096]{1,0:T(8,128)(2,1)}, u32[]{:S(2)}) copy-start(bf16[144,4096]{1,0:T(8,128)(2,1)} %param.18) | copy-start | bytes 3538948
  57.1 46.5 %copy-start.8 = (u32[32]{0:T(128)S(1)}, u32[32]{0:T(128)}, u32[]{:S(2)}) copy-start(u32[32]{0:T(128)} %constant.34) | copy-start | bytes 388
  57.1 64.2 %copy-start.5 = (f32[1152]{0:T(1024)S(1)}, f32[1152]{0:T(1024)}, u32[]{:S(2)}) copy-start(f32[1152]{0:T(1024)} %param.19) | copy-start | bytes 13828
  92.0 8.0 %all-to-all-start.6 = ((f32[8,4,144]{2,1,0:T(4,128)}), f32[8,4,144]{2,1,0:T(4,128)S(1)}, u32[]{:S(2)}, u32[]{:S(2)}) async-start(f32[8,4,144]{2,1,0:T(4,128)} %all_to_all.48), calls=%async_computation.6 | async-start | bytes 65536 | tf_op jit(solution)/shard_map/all_to_all | solution.py:110
  100.0 22.1 %all-to-all-start.4 = ((bf16[144,4,1024]{2,0,1:T(8,128)(2,1)}), bf16[144,4,1024]{2,0,1:T(8,128)(2,1)S(1)}, u32[]{:S(2)}, u32[]{:S(2)}) async-start(bf16[144,4,1024]{2,0,1:T(8,128)(2,1)} %bitcast.42), calls=%async_computation.4 | async-start | bytes 2359296 | tf_op jit(solution)/shard_map/all_to_all | solution.py:100
  103.5 182.8 %all-gather.9.cloned.1.call-start = ((), (), s32[]{:S(2)}) async-start(), calls=%async_computation.7 | async-start | bytes 10616832 | tf_op jit(solution)/shard_map/all_gather | solution.py:175
  122.0 1.1 copy-start.2
  123.2 72.3 %all-to-all-start.3 = ((bf16[4,128,4608]{2,1,0:T(8,128)(2,1)}), bf16[4,128,4608]{2,1,0:T(8,128)(2,1)}, u32[]{:S(2)}, u32[]{:S(2)}) async-start(bf16[4,128,4608]{2,1,0:T(8,128)(2,1)} %bitcast.45), calls=%async_computation.3 | async-start | bytes 9437184 | tf_op jit(solution)/shard_map/all_to_all | solution.py:96
  195.5 58.2 %all-to-all-start.2 = ((bf16[4,128,4608]{2,1,0:T(8,128)(2,1)}), bf16[4,128,4608]{2,1,0:T(8,128)(2,1)}, u32[]{:S(2)}, u32[]{:S(2)}) async-start(bf16[4,128,4608]{2,1,0:T(8,128)(2,1)} %bitcast.46), calls=%async_computation.2 | async-start | bytes 9437184 | tf_op jit(solution)/shard_map/all_to_all | solution.py:96
  200.4 53.2 %collective-permute-start.1 = (bf16[4,128,4608]{2,1,0:T(8,128)(2,1)}, bf16[4,128,4608]{2,1,0:T(8,128)(2,1)}, u32[]{:S(2)}, u32[]{:S(2)}) collective-permute-start(bf16[4,128,4608]{2,1,0:T(8,128)(2,1)} %all-to-all-done.3.refs_1_), channel_id=1, source_target_pairs={{4,0},{0,4},{12,8},{8,12},{20,16},{16,20},{28,24},{24,28},{5,1},{1... | collective-permute-start | bytes 14155784 | tf_op jit(solution)/shard_map/ppermute | solution.py:161
  253.7 8.9 %collective-permute-start = (bf16[4,128,4608]{2,1,0:T(8,128)(2,1)}, bf16[4,128,4608]{2,1,0:T(8,128)(2,1)}, u32[]{:S(2)}, u32[]{:S(2)}) collective-permute-start(bf16[4,128,4608]{2,1,0:T(8,128)(2,1)} %all-to-all-done.2.refs_0_), channel_id=1, source_target_pairs={{4,0},{0,4},{12,8},{8,12},{20,16},{16,20},{28,24},{24,28},{5,1},{1... | collective-permute-start | bytes 14155784 | tf_op jit(solution)/shard_map/ppermute | solution.py:161
Sparse Core Ops, SparseCore 0:
  10.2 95.8 all-gather.12
  107.6 87.8 all-gather.10
  197.1 89.1 all-gather.8

commit v2 on v1

--- a/solution.py
+++ b/solution.py
@@ -72,6 +72,26 @@
     )(*operands)
 
 
+def turn_kernel(rows_ref, out_ref):
+    out_ref[...] = jnp.transpose(rows_ref[...])
+
+
+def turn(rows):
+    height, width = rows.shape
+    stripe = 384 if height % 384 == 0 else 128
+    return pl.pallas_call(
+        turn_kernel,
+        grid=(height // stripe,),
+        in_specs=[pl.BlockSpec((stripe, width), lambda j: (j, 0))],
+        out_specs=pl.BlockSpec((width, stripe), lambda j: (0, j)),
+        out_shape=jax.ShapeDtypeStruct((width, height), rows.dtype),
+        cost_estimate=pl.CostEstimate(
+            flops=0, bytes_accessed=4 * height * width, transcendentals=0
+        ),
+        name="turn",
+    )(rows)
+
+
 def body(
     hidden, positions, key_cache, value_cache, norm_gain, q_proj, k_proj, v_proj, o_proj, post_gain
 ):
@@ -173,7 +193,7 @@
     result = share * multiplier[:, None] * post_gain
     rows_of_group, result = lax.optimization_barrier((rows_of_group, result))
     complete_rows = lax.all_gather(rows_of_group, "rep", axis=0, tiled=True)
-    out_block = jnp.transpose(complete_rows.reshape(model_width, -1))
+    out_block = turn(complete_rows.reshape(model_width, -1))
     return (joined_block, out_block, result.astype(jnp.bfloat16))
 
 

time: 307 us -> 307 us (level)
  local copies, waits for them, and re-layouts: 16.9 us -> 4.25 us
  Pallas kernels: 21.4 us -> 34 us
    unnamed x24 -> x23, local copies, waits for them, and re-layouts: 14.7 us -> 2.05 us
    pallas_call x0 -> x1, Pallas kernels: none -> 12.5 us  [turn(): pl.pallas_call(turn_kernel, grid=(height // stripe,), in_specs=[pl.BlockS...]
where the time goes in v2:
time: 307 us; the launch traced here: 305 us
  waiting for transfers between devices  148 us (48%)
  blocking collectives  66.7 us (22%)
  Pallas kernels  34 us (11%)
  starting transfers between devices  25.7 us (8%)
  between operations  14.6 us (5%)
  matrix products  6.16 us (2%)
  other arithmetic  5.75 us (2%)
  local copies, waits for them, and re-layouts  4.25 us (1%)
    all_gather x2, waiting for transfers between devices, collect(): lax.all_gather(rows[None], 'rep', axis=0, tiled=True, axis_index_groups=g...  67.4 us
    all_to_all x2, waiting for transfers between devices, collect(): return lax.all_to_all(planes, 'tp', split_axis=0, concat_axis=0, tiled=True)  53.2 us
    pallas_call x1, Pallas kernels, join(): pl.pallas_call(functools.partial(join_kernel, per_tp, q_rows, k_rows), gr...  21.4 us
    all_gather x1, blocking collectives, body(): attention_all = lax.all_gather(own_all, 'rep', axis=0, tiled=True)  16.7 us
    all_gather x1, blocking collectives, body(): normed_all = lax.all_gather(normed, 'rep', axis=0, tiled=True)  16.5 us
    unnamed x1, blocking collectives  16 us
    pallas_call x1, Pallas kernels, turn(): pl.pallas_call(turn_kernel, grid=(height // stripe,), in_specs=[pl.BlockS...  12.5 us
    all_to_all x1, blocking collectives, scatter_rows(): lax.all_to_all(wide, 'rep', split_axis=0, concat_axis=0, tiled=True)  10.2 us
  transfers between devices with their start and end apart: 11, of which 7 were waited for; matrix products, arithmetic and copies ran while one was open for 4% of the time, Pallas kernels for 7%

profile of v2, /device:TPU:0, one launch (start us, length us, event | category | flops | bytes accessed | tf_op | source)
XLA Modules:
  0.0 305.3 jit_solution(17895576999306610099)
XLA Ops:
  7.3 2.5 pad_maximum_fusion
  11.6 16.5 %all-gather.3 = bf16[8,4,4608]{2,1,0:T(4,128)(2,1)S(1)} all-gather(bf16[1,4,4608]{2,1,0:T(4,128)(2,1)S(1)} %fusion.9), channel_id=1, replica_groups=mesh['rep'=8,'tp'=4] {'rep'}, dimensions={0}, use_global_device_ids=true | all-gather | bytes 331776 | tf_op jit(solution)/shard_map/all_gather | solution.py:135
  29.9 5.2 %all-to-all-start = ((f32[8,4,256]{2,1,0:T(4,128)}), f32[8,4,256]{2,1,0:T(4,128)}, u32[]{:S(2)}, u32[]{:S(2)}) async-start(f32[8,4,256]{2,1,0:T(4,128)} %reshape.134), calls=%async_computation | async-start | bytes 65536 | tf_op jit(solution)/shard_map/all_to_all | solution.py:126
  35.3 8.2 %all-to-all-done = f32[8,4,256]{2,1,0:T(4,128)} async-done(((f32[8,4,256]{2,1,0:T(4,128)}), f32[8,4,256]{2,1,0:T(4,128)}, u32[]{:S(2)}, u32[]{:S(2)}) %all-to-all-start) | async-done | bytes 32800 | tf_op jit(solution)/shard_map/all_to_all | solution.py:126
  43.4 3.6 %all-to-all-start.1 = ((f32[8,4,256]{2,1,0:T(4,128)}), f32[8,4,256]{2,1,0:T(4,128)S(1)}, u32[]{:S(2)}, u32[]{:S(2)}) async-start(f32[8,4,256]{2,1,0:T(4,128)} %all-to-all-done), calls=%async_computation.1 | async-start | bytes 65536 | tf_op jit(solution)/shard_map/all_to_all | solution.py:130
  47.2 4.7 %all-to-all-done.1 = f32[8,4,256]{2,1,0:T(4,128)S(1)} async-done(((f32[8,4,256]{2,1,0:T(4,128)}), f32[8,4,256]{2,1,0:T(4,128)S(1)}, u32[]{:S(2)}, u32[]{:S(2)}) %all-to-all-start.1) | async-done | bytes 32800 | tf_op jit(solution)/shard_map/all_to_all | solution.py:130
  52.6 3.8 %fusion.15 = (f32[4,4,2]{2,1,0:T(4,128)S(1)}, f32[4,4,2,1024]{3,2,1,0:T(2,128)S(1)}) fusion(bf16[4,4,1024,128]{3,2,1,0:T(8,128)(2,1)} %param.12, bf16[4,4,2,64]{3,2,1,0:T(2,128)(2,1)S(1)} %bitcast.58, bf16[4,4,2,64]{3,2,1,0:T(2,128)(2,1)S(1)} %bitcast.56, pred[4,1024]{1,0:T(4,128)(4,1)S(1)} %iota_compare_fusion), kind=kOutput, calls=%fused_computation.41 | convolution fusion | flops 8536032 | bytes 4337792 | tf_op jit(solution)/shard_map/bkgd,bkld->bkgl/dot_general | solution.py:155
  57.2 7.3 %all_gather.24 = bf16[4,4096]{1,0:T(4,128)(2,1)S(1)} all-gather(bf16[4,1024]{1,0:T(4,128)(2,1)S(1)} %convert_element_type.56), channel_id=1, replica_groups=mesh['rep'=8,'tp'=4] {'tp'}, dimensions={1}, use_global_device_ids=true | all-gather | bytes 40960 | tf_op jit(solution)/shard_map/all_gather | solution.py:183
  64.5 16.7 %all-gather.4 = bf16[8,4,4096]{2,1,0:T(4,128)(2,1)S(1)} all-gather(bf16[1,4,4096]{2,1,0:T(4,128)(2,1)S(1)} %bitcast.53), channel_id=1, replica_groups=mesh['rep'=8,'tp'=4] {'rep'}, dimensions={0}, use_global_device_ids=true | all-gather | bytes 294912 | tf_op jit(solution)/shard_map/all_gather | solution.py:184
  81.7 10.2 %all_to_all.48 = f32[8,4,144]{2,1,0:T(4,128)} all-to-all(f32[8,4,144]{2,1,0:T(4,128)S(1)} %reshape.139), channel_id=1, replica_groups=mesh['rep'=8,'tp'=4] {'rep'}, dimensions={0} | all-to-all | bytes 36864 | tf_op jit(solution)/shard_map/all_to_all | solution.py:126
  92.0 3.3 %all-to-all-start.6 = ((f32[8,4,144]{2,1,0:T(4,128)}), f32[8,4,144]{2,1,0:T(4,128)S(1)}, u32[]{:S(2)}, u32[]{:S(2)}) async-start(f32[8,4,144]{2,1,0:T(4,128)} %all_to_all.48), calls=%async_computation.6 | async-start | bytes 65536 | tf_op jit(solution)/shard_map/all_to_all | solution.py:130
  95.3 1.1 copy.41
  96.4 3.6 %all-to-all-done.6 = f32[8,4,144]{2,1,0:T(4,128)S(1)} async-done(((f32[8,4,144]{2,1,0:T(4,128)}), f32[8,4,144]{2,1,0:T(4,128)S(1)}, u32[]{:S(2)}, u32[]{:S(2)}) %all-to-all-start.6) | async-done | bytes 18464 | tf_op jit(solution)/shard_map/all_to_all | solution.py:130
  100.0 3.5 %all-to-all-start.4 = ((bf16[144,4,1024]{2,0,1:T(8,128)(2,1)}), bf16[144,4,1024]{2,0,1:T(8,128)(2,1)S(1)}, u32[]{:S(2)}, u32[]{:S(2)}) async-start(bf16[144,4,1024]{2,0,1:T(8,128)(2,1)} %bitcast.40), calls=%async_computation.4 | async-start | bytes 2359296 | tf_op jit(solution)/shard_map/all_to_all | solution.py:120
  105.2 16.0 %all-reduce = f32[16]{0:T(128)S(1)} all-reduce(f32[16]{0:T(128)S(1)} %dynamic-update-slice), channel_id=4, replica_groups=mesh['rep'=8,'tp'=4] {'tp'}, use_global_device_ids=true, to_apply=%add | all-reduce | flops 16 | bytes 128
  122.0 1.1 copy-done.2
  123.2 5.0 %all-to-all-start.3 = ((bf16[4,128,4608]{2,1,0:T(8,128)(2,1)}), bf16[4,128,4608]{2,1,0:T(8,128)(2,1)}, u32[]{:S(2)}, u32[]{:S(2)}) async-start(bf16[4,128,4608]{2,1,0:T(8,128)(2,1)} %bitcast.43), calls=%async_computation.3 | async-start | bytes 9437184 | tf_op jit(solution)/shard_map/all_to_all | solution.py:116
  128.1 67.3 %all-gather.11.cloned.1.call-done = bf16[512,4608]{1,0:T(8,128)(2,1)} async-done(((bf16[128,4608]{1,0:T(8,128)(2,1)}), bf16[512,4608]{1,0:T(8,128)(2,1)}) %all-gather.11.cloned.1.call-update) | async-done | bytes 4718608 | tf_op jit(solution)/shard_map/all_gather | solution.py:115
  195.5 4.9 %all-to-all-start.2 = ((bf16[4,128,4608]{2,1,0:T(8,128)(2,1)}), bf16[4,128,4608]{2,1,0:T(8,128)(2,1)}, u32[]{:S(2)}, u32[]{:S(2)}) async-start(bf16[4,128,4608]{2,1,0:T(8,128)(2,1)} %bitcast.44), calls=%async_computation.2 | async-start | bytes 9437184 | tf_op jit(solution)/shard_map/all_to_all | solution.py:116
  200.5 53.2 %all-to-all-done.2.refs_0_ = bf16[4,128,4608]{2,1,0:T(8,128)(2,1)} async-done(((bf16[4,128,4608]{2,1,0:T(8,128)(2,1)}), bf16[4,128,4608]{2,1,0:T(8,128)(2,1)}, u32[]{:S(2)}, u32[]{:S(2)}) %all-to-all-start.2) | async-done | bytes 4718624 | tf_op jit(solution)/shard_map/all_to_all | solution.py:116
  253.7 8.9 %collective-permute-done.refs_2_ = bf16[4,128,4608]{2,1,0:T(8,128)(2,1)} collective-permute-done((bf16[4,128,4608]{2,1,0:T(8,128)(2,1)}, bf16[4,128,4608]{2,1,0:T(8,128)(2,1)}, u32[]{:S(2)}, u32[]{:S(2)}) %collective-permute-start) | collective-permute-done | bytes 4718624 | tf_op jit(solution)/shard_map/ppermute | solution.py:181
  262.5 21.4 %join.1 = bf16[4608,2048]{1,0:T(8,128)(2,1)} custom-call(bf16[4,128,4608]{2,1,0:T(8,128)(2,1)} %all-to-all-done.2.refs_0_, bf16[4,128,4608]{2,1,0:T(8,128)(2,1)} %all-to-all-done.3.refs_1_, bf16[4,128,4608]{2,1,0:T(8,128)(2,1)} %collective-permute-done.refs_2_, bf16[4,128,4608]{2,1,0:T(8,128)(2,1)} %collective-permute-done.1.refs_3_), custom_call_target="tpu_custom_call" | custom-call | bytes 37748736 | tf_op jit(solution)/shard_map/join/pallas_call | solution.py:64
  284.0 2.3 all-gather.9.cloned.1.call-done
  286.3 12.5 %turn.1 = bf16[1024,4608]{1,0:T(8,128)(2,1)} custom-call(bf16[4608,1024]{1,0:T(8,128)(2,1)} %bitcast.42), custom_call_target="tpu_custom_call" | custom-call | bytes 18874368 | tf_op jit(solution)/shard_map/turn/pallas_call | solution.py:82
  (70 shorter events, 8.0 us)
Async XLA Ops:
  7.2 21.0 %copy-start.3 = (bf16[64,4608]{1,0:T(8,128)(2,1)S(1)}, bf16[64,4608]{1,0:T(8,128)(2,1)}, u32[]{:S(2)}) copy-start(bf16[64,4608]{1,0:T(8,128)(2,1)} %param.16) | copy-start | bytes 1769476
  7.2 21.2 %copy-start.4 = (bf16[64,4608]{1,0:T(8,128)(2,1)S(1)}, bf16[64,4608]{1,0:T(8,128)(2,1)}, u32[]{:S(2)}) copy-start(bf16[64,4608]{1,0:T(8,128)(2,1)} %param.17) | copy-start | bytes 1769476
  7.2 21.5 %copy-start.1 = (bf16[128,4608]{1,0:T(8,128)(2,1)S(1)}, bf16[128,4608]{1,0:T(8,128)(2,1)}, u32[]{:S(2)}) copy-start(bf16[128,4608]{1,0:T(8,128)(2,1)} %param.15) | copy-start | bytes 3538948
  7.2 27.9 %copy-start.6 = (s32[4]{0:T(128)S(1)}, s32[4]{0:T(128)}, u32[]{:S(2)}) copy-start(s32[4]{0:T(128)} %param.11) | copy-start | bytes 52
  7.2 116.0 %all-gather.13.cloned.1.call-start = ((), (), s32[]{:S(2)}) async-start(), calls=%async_computation.9 | async-start | bytes 5898240 | tf_op jit(solution)/shard_map/all_gather | solution.py:115
  29.9 13.5 %all-to-all-start = ((f32[8,4,256]{2,1,0:T(4,128)}), f32[8,4,256]{2,1,0:T(4,128)}, u32[]{:S(2)}, u32[]{:S(2)}) async-start(f32[8,4,256]{2,1,0:T(4,128)} %reshape.134), calls=%async_computation | async-start | bytes 65536 | tf_op jit(solution)/shard_map/all_to_all | solution.py:126
  43.4 8.4 %all-to-all-start.1 = ((f32[8,4,256]{2,1,0:T(4,128)}), f32[8,4,256]{2,1,0:T(4,128)S(1)}, u32[]{:S(2)}, u32[]{:S(2)}) async-start(f32[8,4,256]{2,1,0:T(4,128)} %all-to-all-done), calls=%async_computation.1 | async-start | bytes 65536 | tf_op jit(solution)/shard_map/all_to_all | solution.py:130
  47.1 148.4 %all-gather.11.cloned.1.call-start = ((), (), s32[]{:S(2)}) async-start(), calls=%async_computation.8 | async-start | bytes 5898240 | tf_op jit(solution)/shard_map/all_gather | solution.py:115
  52.1 4.2 %copy-start.7 = (bf16[4,4,1024,128]{3,2,1,0:T(8,128)(2,1)S(1)}, bf16[4,4,1024,128]{3,2,1,0:T(8,128)(2,1)}, u32[]{:S(2)}) copy-start(bf16[4,4,1024,128]{3,2,1,0:T(8,128)(2,1)} %param.13) | copy-start | bytes 12582916
  56.3 24.9 %copy-start = (bf16[144,4096]{1,0:T(8,128)(2,1)S(1)}, bf16[144,4096]{1,0:T(8,128)(2,1)}, u32[]{:S(2)}) copy-start(bf16[144,4096]{1,0:T(8,128)(2,1)} %param.18) | copy-start | bytes 3538948
  57.1 46.5 %copy-start.8 = (u32[32]{0:T(128)S(1)}, u32[32]{0:T(128)}, u32[]{:S(2)}) copy-start(u32[32]{0:T(128)} %constant.34) | copy-start | bytes 388
  57.1 64.2 %copy-start.5 = (f32[1152]{0:T(1024)S(1)}, f32[1152]{0:T(1024)}, u32[]{:S(2)}) copy-start(f32[1152]{0:T(1024)} %param.19) | copy-start | bytes 13828
  92.0 8.0 %all-to-all-start.6 = ((f32[8,4,144]{2,1,0:T(4,128)}), f32[8,4,144]{2,1,0:T(4,128)S(1)}, u32[]{:S(2)}, u32[]{:S(2)}) async-start(f32[8,4,144]{2,1,0:T(4,128)} %all_to_all.48), calls=%async_computation.6 | async-start | bytes 65536 | tf_op jit(solution)/shard_map/all_to_all | solution.py:130
  100.0 22.1 %all-to-all-start.4 = ((bf16[144,4,1024]{2,0,1:T(8,128)(2,1)}), bf16[144,4,1024]{2,0,1:T(8,128)(2,1)S(1)}, u32[]{:S(2)}, u32[]{:S(2)}) async-start(bf16[144,4,1024]{2,0,1:T(8,128)(2,1)} %bitcast.40), calls=%async_computation.4 | async-start | bytes 2359296 | tf_op jit(solution)/shard_map/all_to_all | solution.py:120
  103.5 182.8 %all-gather.9.cloned.1.call-start = ((), (), s32[]{:S(2)}) async-start(), calls=%async_computation.7 | async-start | bytes 10616832 | tf_op jit(solution)/shard_map/all_gather | solution.py:195
  122.0 1.1 copy-start.2
  123.2 72.3 %all-to-all-start.3 = ((bf16[4,128,4608]{2,1,0:T(8,128)(2,1)}), bf16[4,128,4608]{2,1,0:T(8,128)(2,1)}, u32[]{:S(2)}, u32[]{:S(2)}) async-start(bf16[4,128,4608]{2,1,0:T(8,128)(2,1)} %bitcast.43), calls=%async_computation.3 | async-start | bytes 9437184 | tf_op jit(solution)/shard_map/all_to_all | solution.py:116
  195.5 58.2 %all-to-all-start.2 = ((bf16[4,128,4608]{2,1,0:T(8,128)(2,1)}), bf16[4,128,4608]{2,1,0:T(8,128)(2,1)}, u32[]{:S(2)}, u32[]{:S(2)}) async-start(bf16[4,128,4608]{2,1,0:T(8,128)(2,1)} %bitcast.44), calls=%async_computation.2 | async-start | bytes 9437184 | tf_op jit(solution)/shard_map/all_to_all | solution.py:116
  200.4 53.2 %collective-permute-start.1 = (bf16[4,128,4608]{2,1,0:T(8,128)(2,1)}, bf16[4,128,4608]{2,1,0:T(8,128)(2,1)}, u32[]{:S(2)}, u32[]{:S(2)}) collective-permute-start(bf16[4,128,4608]{2,1,0:T(8,128)(2,1)} %all-to-all-done.3.refs_1_), channel_id=1, source_target_pairs={{4,0},{0,4},{12,8},{8,12},{20,16},{16,20},{28,24},{24,28},{5,1},{1... | collective-permute-start | bytes 14155784 | tf_op jit(solution)/shard_map/ppermute | solution.py:181
  253.7 8.9 %collective-permute-start = (bf16[4,128,4608]{2,1,0:T(8,128)(2,1)}, bf16[4,128,4608]{2,1,0:T(8,128)(2,1)}, u32[]{:S(2)}, u32[]{:S(2)}) collective-permute-start(bf16[4,128,4608]{2,1,0:T(8,128)(2,1)} %all-to-all-done.2.refs_0_), channel_id=1, source_target_pairs={{4,0},{0,4},{12,8},{8,12},{20,16},{16,20},{28,24},{24,28},{5,1},{1... | collective-permute-start | bytes 14155784 | tf_op jit(solution)/shard_map/ppermute | solution.py:181
Sparse Core Ops, SparseCore 0:
  10.2 95.8 all-gather.12
  107.6 87.8 all-gather.10
  197.1 89.1 all-gather.8
